TPU v7x, 32 devices: a whole 2x2x4 slice. The times are simulated.
32 devices in a mesh: dp: 8 (over z, x), var: 4 (over y, core).
Axes of the slice: x: 2, y: 2, z: 4, core: 2. Of those that a mesh axis runs over, the one named last changes fastest.
Arguments:
- pixels: bfloat16 [8, 24, 4, 256], P('dp', 'var'), may hold values from -6 to 6
- var_ids: int32 [8, 24], P('dp', 'var'), may hold values from 0 to 90, as said below
- counts: int32 [8], P('dp'), may hold values from 3 to 24, as said below
- patch_weight: bfloat16 [91, 4, 1024], replicated, may hold values from -3 to 3
- var_embed: bfloat16 [91, 1024], replicated, may hold values from -5 to 5
- norm_gain: float32 [1024], replicated, may hold values from 0.1 to 1.9
- norm_bias: float32 [1024], replicated, may hold values from -3 to 3
- key_weight: bfloat16 [1024, 1024], P('dp'), may hold values from -0.1875 to 0.1875
- value_weight: bfloat16 [1024, 1024], P('dp'), may hold values from -0.1875 to 0.1875
- query: float32 [16, 64], replicated, may hold values from -200 to 200
- out_weight: bfloat16 [1024, 1024], replicated, may hold values from -0.1875 to 0.1875
Outputs:
- aggregated: bfloat16 [8, 256, 1024], P('dp', 'var')
Inputs may be any that keep to these rules, and one draw needn't show every extreme that they name: `var_ids`: in each sample the ids of slots below its count are distinct; slots at or past the count are padding with arbitrary ids. `counts`: some sample has exactly min(91, 24) live slots and some has exactly 3.
All inputs are finite; a program needn't handle non-finite values.
Results may differ from a plain program's by a relative error of at most 0.018.
Values may be sent and summed in bfloat16 or wider, within the bound.
A program may use at most 64 MiB of HBM per device.

v0:
```python
import math
import jax
import jax.numpy as jnp
from jax import lax
from jax.sharding import PartitionSpec as P


def on_device(
    pixels,
    var_ids,
    counts,
    patch_weight,
    var_embed,
    norm_gain,
    norm_bias,
    key_weight,
    value_weight,
    query,
    out_weight,
):
    slots = pixels.shape[1]
    patches = pixels.shape[3]
    width = out_weight.shape[0]
    heads = query.shape[0]
    head_size = query.shape[1]
    ids = var_ids[0]
    table = patch_weight[ids]
    embedded = jnp.einsum("skp,skd->spd", pixels[0], table, preferred_element_type=jnp.float32)
    embedded = embedded + var_embed[ids].astype(jnp.float32)[:, None, :]
    center = embedded - jnp.mean(embedded, axis=-1, keepdims=True)
    spread = jnp.mean(center * center, axis=-1, keepdims=True)
    normed = (center * lax.rsqrt(spread + 1e-05) * norm_gain + norm_bias).astype(jnp.bfloat16)
    flat = normed.reshape(slots * patches, width)
    local_fold = jnp.einsum(
        "jhe,he->jh",
        key_weight.astype(jnp.float32).reshape(-1, heads, head_size),
        query,
        precision=lax.Precision.HIGHEST,
    )
    folded = lax.all_gather(local_fold, "dp", axis=0, tiled=True)
    values = jnp.dot(
        flat,
        lax.all_gather(value_weight, "dp", axis=0, tiled=True),
        preferred_element_type=jnp.float32,
    )
    scores = jnp.dot(flat.astype(jnp.float32), folded, precision=lax.Precision.HIGHEST)
    scores = (scores * (1.0 / math.sqrt(head_size))).reshape(slots, patches, heads)
    first_slot = lax.axis_index("var") * slots
    live = (first_slot + jnp.arange(slots, dtype=jnp.int32) < counts[0])[:, None, None]
    scores = jnp.where(live, scores, jnp.float32(-1e30))
    values = values.astype(jnp.bfloat16).reshape(slots, patches, width)
    values_all = lax.all_to_all(values, "var", split_axis=1, concat_axis=0, tiled=True)
    scores_all = lax.all_to_all(scores, "var", split_axis=1, concat_axis=0, tiled=True)
    owned = scores_all.shape[1]
    peak = jnp.max(scores_all, axis=0)
    expo = jnp.exp(scores_all - peak)
    total = jnp.sum(expo, axis=0)
    numer = jnp.einsum(
        "sph,sphe->phe",
        expo.astype(jnp.bfloat16),
        values_all.reshape(-1, owned, heads, head_size),
        preferred_element_type=jnp.float32,
    )
    mixed = (numer / total[:, :, None]).reshape(-1, width).astype(jnp.bfloat16)
    return jnp.dot(mixed, out_weight, preferred_element_type=jnp.float32).astype(jnp.bfloat16)[None]


def solution(mesh):
    placed = (
        P("dp", "var", None, None),
        P("dp", "var"),
        P("dp"),
        P(),
        P(),
        P(),
        P(),
        P("dp", None),
        P("dp", None),
        P(),
        P(),
    )
    return jax.shard_map(
        on_device, mesh=mesh, in_specs=placed, out_specs=P("dp", "var", None), check_vma=False
    )
```

profile of v0, /device:TPU:0, one launch (start us, length us, event | category | flops | bytes accessed | tf_op | source)
XLA Modules:
  0.0 155.5 jit_solution(17821916475907785103)
XLA Ops:
  6.5 0.0 copy-start
  6.5 0.0 all-gather.2.cloned.1.call-start
  6.5 0.7 all-gather.2.cloned.1.call-update
  7.3 0.7 fusion.7
  7.9 1.5 gather_fusion.1
  9.5 1.7 %gather_fusion = bf16[6,4,1024]{2,1,0:T(4,128)(2,1)S(1)} fusion(bf16[91,4,1024]{2,1,0:T(4,128)(2,1)} %param.14, s32[1024]{0:T(1024)S(1)} %pad_clamp_fusion), kind=kCustom, calls=%fused_computation | custom fusion | bytes 98328 | tf_op jit(solution)/shard_map/gather | solution.py:27
  11.2 1.1 copy.28
  12.3 1.0 fusion.8
  13.3 32.6 %all_gather.6 = f32[1024,16]{0,1:T(8,128)S(1)} all-gather(f32[128,16]{0,1:T(8,128)S(1)} %bitcast.71), channel_id=1, replica_groups=mesh['dp'=8,'var'=4] {'dp'}, dimensions={0}, use_global_device_ids=true | all-gather | bytes 73728 | tf_op jit(solution)/shard_map/all_gather | solution.py:40
  45.9 0.0 copy-start.2
  46.0 0.0 copy-start.3
  46.0 1.8 %bitcast_reduce_fusion = (f32[6,256]{1,0:T(8,128)S(1)}, f32[6,1024,256]{1,2,0:T(8,128)S(1)}) fusion(f32[6,1024]{1,0:T(8,128)S(1)} %convert_element_type.27, bf16[6,4,1024]{2,1,0:T(4,128)(2,1)S(1)} %gather_fusion, bf16[1,6,4,256]{3,2,1,0:T(4,128)(2,1)} %param.11), kind=kOutput, calls=%fused_computation.3 | convolution fusion | flops 15727104 | bytes 6383616 | tf_op jit(solution)/shard_map/skp,skd->spd/dot_general | solution.py:28
  47.8 1.0 multiply_reduce_fusion
  48.8 0.0 copy-done.2
  48.8 0.0 copy-done.3
  48.8 1.4 add_convert_fusion
  50.2 0.0 copy-start.1
  50.2 1.7 %copy-done.1 = bf16[6,256,1024]{2,1,0:T(8,128)(2,1)} copy-done((bf16[6,256,1024]{2,1,0:T(8,128)(2,1)}, bf16[6,256,1024]{2,1,0:T(8,128)(2,1)S(1)}, u32[]{:S(2)}) %copy-start.1) | copy-done | bytes 3145752
  51.9 2.5 %convolution_multiply_fusion = f32[1536,16]{0,1:T(8,128)S(1)} fusion(bf16[1536,1024]{1,0:T(8,128)(2,1)S(1)} %bitcast.62, f32[1024,16]{0,1:T(8,128)S(1)} %all_gather.6), kind=kOutput, calls=%fused_computation.9 | convolution fusion | flops 302014464 | bytes 3309568 | tf_op jit(solution)/shard_map/dot_general | solution.py:46
  55.2 0.1 broadcast_select_fusion
  55.2 0.4 copy.29
  55.7 1.0 reshape.95
  56.7 3.3 %all-to-all-start = ((f32[4,1,6144]{2,1,0:T(1,128)}), f32[4,1,6144]{2,1,0:T(1,128)S(1)}, u32[]{:S(2)}, u32[]{:S(2)}) async-start(f32[4,1,6144]{2,1,0:T(1,128)} %reshape.95), calls=%async_computation | async-start | bytes 196608 | tf_op jit(solution)/shard_map/all_to_all | solution.py:53
  60.0 1.5 all-gather.2.cloned.1.call-done
  61.5 6.0 %convolution_convert_fusion = bf16[1536,1024]{1,0:T(8,128)(2,1)S(1)} fusion(bf16[1536,1024]{1,0:T(8,128)(2,1)} %bitcast.63, bf16[1024,1024]{1,0:T(8,128)(2,1)} %all-gather.2.cloned.1.call-done), kind=kOutput, calls=%fused_computation.8 | convolution fusion | flops 3222798336 | bytes 8388608 | tf_op jit(solution)/shard_map/dot_general | solution.py:41
  67.5 3.8 %copy.32 = bf16[6,256,1024]{2,0,1:T(8,128)(2,1)} copy(bf16[6,256,1024]{2,1,0:T(8,128)(2,1)S(1)} %bitcast.66) | data formatting | bytes 6291456 | tf_op jit(solution)/shard_map/reshape | solution.py:51
  71.2 0.0 all-to-all-done
  71.2 5.0 %all-to-all-start.1 = ((bf16[6,256,1024]{2,0,1:T(8,128)(2,1)}), bf16[6,256,1024]{2,0,1:T(8,128)(2,1)}, u32[]{:S(2)}, u32[]{:S(2)}) async-start(bf16[6,256,1024]{2,0,1:T(8,128)(2,1)} %copy.32), calls=%async_computation.1 | async-start | bytes 8388608 | tf_op jit(solution)/shard_map/all_to_all | solution.py:52
  76.3 0.5 broadcast.67
  76.8 0.9 reduce.2
  77.7 0.5 reshape.96
  78.2 0.3 copy.41
  78.5 0.1 bitcast_reduce_fusion.1
  78.6 0.5 copy.38
  79.2 0.1 exponential_reduce_fusion
  79.3 0.1 copy.35
  79.4 44.9 %all-to-all-done.1 = bf16[6,256,1024]{2,0,1:T(8,128)(2,1)} async-done(((bf16[6,256,1024]{2,0,1:T(8,128)(2,1)}), bf16[6,256,1024]{2,0,1:T(8,128)(2,1)}, u32[]{:S(2)}, u32[]{:S(2)}) %all-to-all-start.1) | async-done | bytes 3145760 | tf_op jit(solution)/shard_map/all_to_all | solution.py:52
  124.3 5.6 %copy.34 = bf16[4,6,64,1024]{3,2,1,0:T(8,128)(2,1)} copy(bf16[4,6,64,1024]{3,1,2,0:T(8,128)(2,1)} %bitcast.19) | data formatting | bytes 6291456 | tf_op jit(solution)/shard_map/all_to_all | solution.py:52
  129.9 9.2 %reshape.74 = bf16[24,64,16,64]{3,2,1,0:T(8,128)(2,1)} reshape(bf16[4,6,64,1024]{3,2,1,0:T(8,128)(2,1)} %copy.34) | data formatting | bytes 6291456 | tf_op jit(solution)/shard_map/reshape | solution.py:61
  139.1 8.0 %fusion = f32[64,16,1,64]{3,2,1,0:T(1,128)S(1)} fusion(bf16[24,64,16,1]{0,3,2,1:T(2,128)(2,1)S(1)} %copy.38, bf16[24,64,16,64]{3,2,1,0:T(8,128)(2,1)} %reshape.74), kind=kOutput, calls=%fused_computation.4 | convolution fusion | flops 3145728 | bytes 3457024 | tf_op jit(solution)/shard_map/sph,sphe->phe/dot_general | solution.py:58
  147.1 0.2 divide_convert_fusion
  147.3 0.2 convert_element_type.32
  147.5 0.0 copy-done
  147.5 1.1 fusion.2
  (8 shorter events, 0.1 us)
Async XLA Ops:
  6.5 141.0 %copy-start = (bf16[1024,1024]{1,0:T(8,128)(2,1)S(1)}, bf16[1024,1024]{1,0:T(8,128)(2,1)}, u32[]{:S(2)}) copy-start(bf16[1024,1024]{1,0:T(8,128)(2,1)} %param.21) | copy-start | bytes 6291460
  6.5 54.9 %all-gather.2.cloned.1.call-start = ((), (), s32[]{:S(2)}) async-start(), calls=%async_computation.2 | async-start | bytes 2359296 | tf_op jit(solution)/shard_map/all_gather | solution.py:43
  45.9 2.9 %copy-start.2 = (f32[1024]{0:T(1024)S(1)}, f32[1024]{0:T(1024)}, u32[]{:S(2)}) copy-start(f32[1024]{0:T(1024)} %param.17) | copy-start | bytes 12292
  46.0 2.9 %copy-start.3 = (f32[1024]{0:T(1024)S(1)}, f32[1024]{0:T(1024)}, u32[]{:S(2)}) copy-start(f32[1024]{0:T(1024)} %param.16) | copy-start | bytes 12292
  50.2 1.7 %copy-start.1 = (bf16[6,256,1024]{2,1,0:T(8,128)(2,1)}, bf16[6,256,1024]{2,1,0:T(8,128)(2,1)S(1)}, u32[]{:S(2)}) copy-start(bf16[6,256,1024]{2,1,0:T(8,128)(2,1)S(1)} %add_convert_fusion) | copy-start | bytes 9437188
  56.7 14.5 %all-to-all-start = ((f32[4,1,6144]{2,1,0:T(1,128)}), f32[4,1,6144]{2,1,0:T(1,128)S(1)}, u32[]{:S(2)}, u32[]{:S(2)}) async-start(f32[4,1,6144]{2,1,0:T(1,128)} %reshape.95), calls=%async_computation | async-start | bytes 196608 | tf_op jit(solution)/shard_map/all_to_all | solution.py:53
  71.2 53.1 %all-to-all-start.1 = ((bf16[6,256,1024]{2,0,1:T(8,128)(2,1)}), bf16[6,256,1024]{2,0,1:T(8,128)(2,1)}, u32[]{:S(2)}, u32[]{:S(2)}) async-start(bf16[6,256,1024]{2,0,1:T(8,128)(2,1)} %copy.32), calls=%async_computation.1 | async-start | bytes 8388608 | tf_op jit(solution)/shard_map/all_to_all | solution.py:52
Sparse Core Ops, SparseCore 0:
  9.5 51.9 all-gather.1
where the time goes:
time: 156 us; the launch traced here: 155 us
  waiting for transfers between devices  47.1 us (30%)
  blocking collectives  32.6 us (21%)
  local copies, waits for them, and re-layouts  28.3 us (18%)
  matrix products  20.4 us (13%)
  between operations  14.2 us (9%)
  starting transfers between devices  8.35 us (5%)
  other arithmetic  4.48 us (3%)
    all_to_all x1, waiting for transfers between devices, on_device(): lax.all_to_all(values, 'var', split_axis=1, concat_axis=0, tiled=True)  44.9 us
    all_gather x1, blocking collectives, on_device(): folded = lax.all_gather(local_fold, 'dp', axis=0, tiled=True)  32.6 us
    reshape x1, local copies, waits for them, and re-layouts, on_device(): values_all.reshape(-1, owned, heads, head_size)  9.19 us
    dot_general x1, matrix products, on_device(): jnp.einsum('sph,sphe->phe', expo.astype(jnp.bfloat16), values_all.reshape...  7.95 us
    dot_general x1, matrix products, on_device(): jnp.dot(flat, lax.all_gather(value_weight, 'dp', axis=0, tiled=True), pre...  5.98 us
    all_to_all x1, local copies, waits for them, and re-layouts, on_device(): lax.all_to_all(values, 'var', split_axis=1, concat_axis=0, tiled=True)  5.62 us
    all_to_all x1, starting transfers between devices, on_device(): lax.all_to_all(values, 'var', split_axis=1, concat_axis=0, tiled=True)  5.04 us
    unnamed x11, local copies, waits for them, and re-layouts  4.28 us
  transfers between devices with their start and end apart: 3, of which 2 were waited for; matrix products, arithmetic and copies ran while one was open for 17% of the time, Pallas kernels for 0%

commit v1 on v0

--- a/solution.py
+++ b/solution.py
@@ -49,7 +49,10 @@
     live = (first_slot + jnp.arange(slots, dtype=jnp.int32) < counts[0])[:, None, None]
     scores = jnp.where(live, scores, jnp.float32(-1e30))
     values = values.astype(jnp.bfloat16).reshape(slots, patches, width)
-    values_all = lax.all_to_all(values, "var", split_axis=1, concat_axis=0, tiled=True)
+    values_all = jnp.concatenate(
+        lax.all_to_all(jnp.stack(jnp.split(values, lax.axis_size("var"), axis=1)), "var", 0, 0),
+        axis=0,
+    )
     scores_all = lax.all_to_all(scores, "var", split_axis=1, concat_axis=0, tiled=True)
     owned = scores_all.shape[1]
     peak = jnp.max(scores_all, axis=0)

time: 156 us -> 138 us (0.88)
  waiting for transfers between devices: 47.1 us -> 35.9 us
  local copies, waits for them, and re-layouts: 28.3 us -> 19.2 us
  other arithmetic: 4.48 us -> 6.38 us
    reshape x2 -> x0, local copies, waits for them, and re-layouts: 13 us -> none  [the longest x1 9.19 us: on_device(): values_all.reshape(-1, owned, heads, head_size)]
    all_to_all x1, waiting for transfers between devices: 44.9 us -> 33.7 us  [on_device(): lax.all_to_all(jnp.stack(jnp.split(values, lax.axis_size('var'), axis=1))...]
    another operation x0 -> x2, local copies, waits for them, and re-layouts: none -> 9.5 us  [the longest x1 9.19 us: on_device(): values_all.reshape(-1, owned, heads, head_size)]
    all_to_all x1 -> x0, local copies, waits for them, and re-layouts: 5.62 us -> none  [on_device(): lax.all_to_all(values, 'var', split_axis=1, concat_axis=0, tiled=True)]
    another operation x0 -> x1, other arithmetic: none -> 1.89 us  [on_device(): jnp.stack(jnp.split(values, lax.axis_size('var'), axis=1))]
  transfers between devices with their start and end apart: 3 -> 3, of which waited for: 2 -> 2; matrix products, arithmetic and copies ran while one was open for 17% -> 19% of each run, Pallas kernels for 0% -> 0%
where the time goes in v1:
time: 138 us; the launch traced here: 137 us
  waiting for transfers between devices  35.9 us (26%)
  blocking collectives  32.6 us (24%)
  matrix products  20.4 us (15%)
  local copies, waits for them, and re-layouts  19.2 us (14%)
  between operations  14.3 us (10%)
  starting transfers between devices  8.14 us (6%)
  other arithmetic  6.38 us (5%)
    all_to_all x1, waiting for transfers between devices, on_device(): lax.all_to_all(jnp.stack(jnp.split(values, lax.axis_size('var'), axis=1))...  33.7 us
    all_gather x1, blocking collectives, on_device(): folded = lax.all_gather(local_fold, 'dp', axis=0, tiled=True)  32.6 us
    another operation x1, local copies, waits for them, and re-layouts, on_device(): values_all.reshape(-1, owned, heads, head_size)  9.19 us
    dot_general x1, matrix products, on_device(): jnp.einsum('sph,sphe->phe', expo.astype(jnp.bfloat16), values_all.reshape...  7.95 us
    dot_general x1, matrix products, on_device(): jnp.dot(flat, lax.all_gather(value_weight, 'dp', axis=0, tiled=True), pre...  5.98 us
    all_to_all x1, starting transfers between devices, on_device(): lax.all_to_all(jnp.stack(jnp.split(values, lax.axis_size('var'), axis=1))...  4.83 us
    unnamed x11, local copies, waits for them, and re-layouts  4.29 us
    all_to_all x1, starting transfers between devices, on_device(): lax.all_to_all(scores, 'var', split_axis=1, concat_axis=0, tiled=True)  3.3 us
  transfers between devices with their start and end apart: 3, of which 2 were waited for; matrix products, arithmetic and copies ran while one was open for 19% of the time, Pallas kernels for 0%

profile of v1, /device:TPU:0, one launch (start us, length us, event | category | flops | bytes accessed | tf_op | source)
XLA Modules:
  0.0 136.9 jit_solution(1398388512857979157)
XLA Ops:
  6.5 0.0 copy-start
  6.5 0.0 all-gather.2.cloned.1.call-start
  6.5 0.7 all-gather.2.cloned.1.call-update
  7.3 0.7 fusion.7
  7.9 1.5 %gather_fusion.1 = bf16[6,1024]{1,0:T(8,128)(2,1)S(1)} fusion(bf16[91,1024]{1,0:T(8,128)(2,1)} %param.15, s32[1024]{0:T(1024)S(1)} %pad_clamp_fusion), kind=kCustom, calls=%fused_computation.1 | custom fusion | bytes 24600 | tf_op jit(solution)/shard_map/gather | solution.py:29
  9.5 1.7 %gather_fusion = bf16[6,4,1024]{2,1,0:T(4,128)(2,1)S(1)} fusion(bf16[91,4,1024]{2,1,0:T(4,128)(2,1)} %param.14, s32[1024]{0:T(1024)S(1)} %pad_clamp_fusion), kind=kCustom, calls=%fused_computation | custom fusion | bytes 98328 | tf_op jit(solution)/shard_map/gather | solution.py:27
  11.2 1.1 copy.21
  12.3 1.0 fusion.8
  13.3 32.6 %all_gather.6 = f32[1024,16]{0,1:T(8,128)S(1)} all-gather(f32[128,16]{0,1:T(8,128)S(1)} %bitcast.76), channel_id=1, replica_groups=mesh['dp'=8,'var'=4] {'dp'}, dimensions={0}, use_global_device_ids=true | all-gather | bytes 73728 | tf_op jit(solution)/shard_map/all_gather | solution.py:40
  45.9 1.8 %bitcast_reduce_fusion = (f32[6,256]{1,0:T(8,128)S(1)}, f32[6,1024,256]{1,2,0:T(8,128)S(1)}) fusion(f32[6,1024]{1,0:T(8,128)S(1)} %convert_element_type.27, bf16[6,4,1024]{2,1,0:T(4,128)(2,1)S(1)} %gather_fusion, bf16[1,6,4,256]{3,2,1,0:T(4,128)(2,1)} %param.11), kind=kOutput, calls=%fused_computation.3 | convolution fusion | flops 15727104 | bytes 6383616 | tf_op jit(solution)/shard_map/skp,skd->spd/dot_general | solution.py:28
  47.8 0.0 copy-start.2
  47.8 0.0 copy-start.3
  47.8 1.0 multiply_reduce_fusion
  48.8 0.0 copy-done.2
  48.8 0.0 copy-done.3
  48.8 1.4 %add_convert_fusion = bf16[6,256,1024]{2,1,0:T(8,128)(2,1)S(1)} fusion(f32[6,1024,256]{1,2,0:T(8,128)S(1)} %get-tuple-element.10, f32[1024]{0:T(1024)S(1)} %copy-done.2, f32[1024]{0:T(1024)S(1)} %copy-done.3, f32[6,256]{1,0:T(8,128)S(1)} %add_rsqrt_fusion, f32[6,256]{1,0:T(8,128)S(1)} %broadcast_multiply_fusion, f32[6,1024]{1,0:T(8,128)S(1)} %convert_element_type.27), kind=kLoop, calls=%fused_computation.6 | loop fusion | flops 9437184 | bytes 9482240 | tf_op jit(solution)/shard_map/convert_element_type | solution.py:32
  50.2 0.0 copy-start.1
  50.3 1.7 %copy-done.1 = bf16[6,256,1024]{2,1,0:T(8,128)(2,1)} copy-done((bf16[6,256,1024]{2,1,0:T(8,128)(2,1)}, bf16[6,256,1024]{2,1,0:T(8,128)(2,1)S(1)}, u32[]{:S(2)}) %copy-start.1) | copy-done | bytes 3145752
  51.9 2.5 %convolution_multiply_fusion = f32[1536,16]{0,1:T(8,128)S(1)} fusion(bf16[1536,1024]{1,0:T(8,128)(2,1)S(1)} %bitcast.67, f32[1024,16]{0,1:T(8,128)S(1)} %all_gather.6), kind=kOutput, calls=%fused_computation.10 | convolution fusion | flops 302014464 | bytes 3309568 | tf_op jit(solution)/shard_map/dot_general | solution.py:46
  55.2 0.1 broadcast_select_fusion
  55.2 0.4 copy.22
  55.7 1.0 reshape.90
  56.7 3.3 %all-to-all-start = ((f32[4,1,6144]{2,1,0:T(1,128)}), f32[4,1,6144]{2,1,0:T(1,128)S(1)}, u32[]{:S(2)}, u32[]{:S(2)}) async-start(f32[4,1,6144]{2,1,0:T(1,128)} %reshape.90), calls=%async_computation | async-start | bytes 196608 | tf_op jit(solution)/shard_map/all_to_all | solution.py:56
  60.0 1.4 %all-gather.2.cloned.1.call-done = bf16[1024,1024]{1,0:T(8,128)(2,1)} async-done(((bf16[128,1024]{1,0:T(8,128)(2,1)}), bf16[1024,1024]{1,0:T(8,128)(2,1)}) %all-gather.2.cloned.1.call-update) | async-done | bytes 2097168 | tf_op jit(solution)/shard_map/all_gather | solution.py:43
  61.5 6.0 %convolution_convert_fusion = bf16[1536,1024]{1,0:T(8,128)(2,1)S(1)} fusion(bf16[1536,1024]{1,0:T(8,128)(2,1)} %bitcast.68, bf16[1024,1024]{1,0:T(8,128)(2,1)} %all-gather.2.cloned.1.call-done), kind=kOutput, calls=%fused_computation.8 | convolution fusion | flops 3222798336 | bytes 8388608 | tf_op jit(solution)/shard_map/dot_general | solution.py:41
  67.5 0.3 slice_bitcast_fusion.3
  67.8 1.9 %pad_maximum_fusion = bf16[4,6,64,1024]{3,2,1,0:T(8,128)(2,1)} fusion(bf16[1,6,64,1024]{3,2,1,0:T(8,128)(2,1)S(1)} %get-tuple-element.6, bf16[1,6,64,1024]{3,2,1,0:T(8,128)(2,1)S(1)} %get-tuple-element.7, bf16[1,6,64,1024]{3,2,1,0:T(8,128)(2,1)S(1)} %get-tuple-element.8, bf16[1,6,64,1024]{3,2,1,0:T(8,128)(2,1)S(1)} %get-tuple-element.5), kind=kLoop, calls=%fused_computation.9 | loop fusion | flops 4718592 | bytes 6291456 | tf_op jit(solution)/shard_map/stack | solution.py:53
  69.7 0.0 all-to-all-done
  69.7 4.8 %all-to-all-start.1 = ((bf16[4,6,64,1024]{3,2,1,0:T(8,128)(2,1)}), bf16[4,6,64,1024]{3,2,1,0:T(8,128)(2,1)}, u32[]{:S(2)}, u32[]{:S(2)}) async-start(bf16[4,6,64,1024]{3,2,1,0:T(8,128)(2,1)} %pad_maximum_fusion), calls=%async_computation.1 | async-start | bytes 6291456 | tf_op jit(solution)/shard_map/all_to_all | solution.py:53
  74.5 0.5 broadcast.67
  75.0 0.9 reduce.2
  75.9 0.5 reshape.91
  76.4 0.3 copy.31
  76.7 0.1 bitcast_reduce_fusion.1
  76.8 0.5 copy.28
  77.4 0.1 exponential_reduce_fusion
  77.5 0.1 copy.25
  77.6 33.7 %all-to-all-done.1 = bf16[4,6,64,1024]{3,2,1,0:T(8,128)(2,1)} async-done(((bf16[4,6,64,1024]{3,2,1,0:T(8,128)(2,1)}), bf16[4,6,64,1024]{3,2,1,0:T(8,128)(2,1)}, u32[]{:S(2)}, u32[]{:S(2)}) %all-to-all-start.1) | async-done | bytes 3145760 | tf_op jit(solution)/shard_map/all_to_all | solution.py:53
  111.3 9.2 %reshape_reshape.3 = bf16[24,64,16,64]{3,2,1,0:T(8,128)(2,1)} reshape(bf16[4,6,64,1024]{3,2,1,0:T(8,128)(2,1)} %all-to-all-done.1) | data formatting | bytes 6291456 | tf_op jit(solution)/shard_map/reshape;reshape | solution.py:64
  120.5 8.0 %fusion = f32[64,16,1,64]{3,2,1,0:T(1,128)S(1)} fusion(bf16[24,64,16,1]{0,3,2,1:T(2,128)(2,1)S(1)} %copy.28, bf16[24,64,16,64]{3,2,1,0:T(8,128)(2,1)} %reshape_reshape.3), kind=kOutput, calls=%fused_computation.4 | convolution fusion | flops 3145728 | bytes 3457024 | tf_op jit(solution)/shard_map/sph,sphe->phe/dot_general | solution.py:61
  128.4 0.2 divide_convert_fusion
  128.7 0.2 convert_element_type.32
  128.9 0.0 copy-done
  128.9 1.1 fusion.2
  (8 shorter events, 0.1 us)
Async XLA Ops:
  6.5 122.3 %copy-start = (bf16[1024,1024]{1,0:T(8,128)(2,1)S(1)}, bf16[1024,1024]{1,0:T(8,128)(2,1)}, u32[]{:S(2)}) copy-start(bf16[1024,1024]{1,0:T(8,128)(2,1)} %param.21) | copy-start | bytes 6291460
  6.5 54.9 %all-gather.2.cloned.1.call-start = ((), (), s32[]{:S(2)}) async-start(), calls=%async_computation.2 | async-start | bytes 2359296 | tf_op jit(solution)/shard_map/all_gather | solution.py:43
  47.8 1.0 copy-start.2
  47.8 1.0 copy-start.3
  50.2 1.7 %copy-start.1 = (bf16[6,256,1024]{2,1,0:T(8,128)(2,1)}, bf16[6,256,1024]{2,1,0:T(8,128)(2,1)S(1)}, u32[]{:S(2)}) copy-start(bf16[6,256,1024]{2,1,0:T(8,128)(2,1)S(1)} %add_convert_fusion) | copy-start | bytes 9437188
  56.7 13.0 %all-to-all-start = ((f32[4,1,6144]{2,1,0:T(1,128)}), f32[4,1,6144]{2,1,0:T(1,128)S(1)}, u32[]{:S(2)}, u32[]{:S(2)}) async-start(f32[4,1,6144]{2,1,0:T(1,128)} %reshape.90), calls=%async_computation | async-start | bytes 196608 | tf_op jit(solution)/shard_map/all_to_all | solution.py:56
  69.7 41.6 %all-to-all-start.1 = ((bf16[4,6,64,1024]{3,2,1,0:T(8,128)(2,1)}), bf16[4,6,64,1024]{3,2,1,0:T(8,128)(2,1)}, u32[]{:S(2)}, u32[]{:S(2)}) async-start(bf16[4,6,64,1024]{3,2,1,0:T(8,128)(2,1)} %pad_maximum_fusion), calls=%async_computation.1 | async-start | bytes 6291456 | tf_op jit(solution)/shard_map/all_to_all | solution.py:53
Sparse Core Ops, SparseCore 0:
  9.5 51.9 all-gather.1
